TPU v7x, 512 devices: a whole 4x8x8 slice. The times are simulated.
512 devices in a mesh: row: 16 (over x, y_lo), col: 32 (over z, y_hi, core).
Axes of the slice: x: 4, y: 8 (y_hi: 2, y_lo: 4; y = y_hi * 4 + y_lo), z: 8, core: 2. Of those that a mesh axis runs over, the one named last changes fastest.
Arguments:
- object_field: float32 [2, 4096, 8192], P(None, 'row', 'col'), may hold values from -5 to 5
- velocity: float32 [2, 4096, 8192], P(None, 'row', 'col'), may hold values from -5 to 5
- positions: int32 [16, 32, 1, 2], P('row', 'col'), may hold values from 0 to 128
- measured: float32 [16, 32, 1, 256, 256], P('row', 'col'), may hold values from 0 to 2
- probe: float32 [2, 256, 256], replicated, may hold values from -5 to 5
Outputs:
- object_out: float32 [2, 4096, 8192], P(None, 'row', 'col')
- velocity_out: float32 [2, 4096, 8192], P(None, 'row', 'col')
All inputs are finite; a program needn't handle non-finite values.
Results may differ from a plain program's by a relative error of at most 0.00018.
Values sent between devices are 32-bit elements; how exact they have to be, the bound alone decides.
A program may use at most 64 MiB of HBM per device.

v0:
```python
import functools

import numpy as np

import jax
import jax.numpy as jnp
from jax import lax
from jax.experimental import pallas as pl
from jax.experimental.pallas import tpu as pltpu
from jax.sharding import PartitionSpec as P

N = 256
W = 128
ITERS = 2
STEP = 0.1
MOMENTUM = 0.8
MESH = pl.DeviceIdType.MESH
F32 = jnp.float32
BF16 = jnp.bfloat16

UP, DOWN, TO_LEFT, TO_RIGHT = (-1, 0), (1, 0), (0, -1), (0, 1)
MESSAGES = {
    "obj_ht": TO_LEFT, "obj_hb": TO_LEFT, "obj_vr": UP, "obj_vl": UP,
    "grad_vl": DOWN, "grad_vr": DOWN, "grad_hb": TO_RIGHT, "grad_ht": TO_RIGHT,
    "next_vr": UP, "next_hb": TO_LEFT, "next_ht": TO_LEFT, "next_vl": UP,
    "last_vl": DOWN, "last_vr": DOWN, "last_hb": TO_RIGHT, "last_ht": TO_RIGHT,
}
SLOT = {name: i for i, name in enumerate(MESSAGES)}
TOP, BOTTOM = pl.ds(0, W), pl.ds(W, W)
LEFT, RIGHT = pl.ds(0, W), pl.ds(W, W)


CFG = dict(R1pre="tr", R1post="b", mid="|bB", mid2="hHrR", R4pre="|r", R4post="b", sweep="bt")


def fourier_tables():
    index = np.arange(N)
    angle = -2.0 * np.pi * (index[:, None] * index[None, :] % N) / N
    parts = []
    for table in (np.cos(angle) / np.sqrt(N), np.sin(angle) / np.sqrt(N)):
        high = table.astype(BF16)
        parts += [high, (table - high.astype(np.float64)).astype(BF16)]
    return np.stack(parts)


def split(value):
    high = value.astype(BF16)
    return high, (value - high.astype(F32)).astype(BF16)


def kernel(
    n_rows, n_cols,
    pos_hbm, obj_hbm, vel_hbm, meas_hbm, probe_hbm, table_hbm,
    obj_out, vel_out,
    pos, obj, vel, obj1, vel1, meas, probe, table, right_table, left_table,
    stack, stack2, grad, halo, recv, send, place, place_in,
    load_sem, store_sem, send_sem, recv_sem, place_send, place_recv,
):
    r = lax.axis_index("row")
    c = lax.axis_index("col")
    has = {UP: r > 0, DOWN: r < n_rows - 1, TO_LEFT: c > 0, TO_RIGHT: c < n_cols - 1}

    barrier = pltpu.get_barrier_semaphore()
    for (dr, dc), there in has.items():
        @pl.when(there)
        def _():
            pl.semaphore_signal(barrier, inc=1, device_id=(r + dr, c + dc), device_id_type=MESH)

    loads = [
        pltpu.make_async_copy(src, dst, load_sem.at[i])
        for i, (src, dst) in enumerate([
            (pos_hbm, pos), (obj_hbm, obj), (table_hbm, table), (probe_hbm, probe),
            (meas_hbm, meas), (vel_hbm, vel),
        ])
    ]
    for load in loads:
        load.start()

    zeros = jnp.zeros((2, W, W), F32)
    for way in (UP, DOWN, TO_LEFT, TO_RIGHT):
        @pl.when(~has[-way[0], -way[1]])
        def _():
            for name, to in MESSAGES.items():
                if to == way:
                    recv[SLOT[name]] = zeros

    @pl.when(~has[UP])
    def _():
        place_in[...] = jnp.zeros((8, W), F32)

    loads[0].wait()
    dy = pos[0]
    dx = pos[1]
    rows = lax.broadcasted_iota(jnp.int32, (W, W), 0)
    cols = lax.broadcasted_iota(jnp.int32, (W, W), 1)
    below = rows < dy
    beside = cols < dx
    place[...] = jnp.full((8, W), dx.astype(F32))

    with jax.named_scope("wait_barrier"):
        pl.semaphore_wait(barrier, sum(there.astype(jnp.int32) for there in has.values()))

    started = {}

    def message(name, src):
        dr, dc = MESSAGES[name]
        i = SLOT[name]
        return pltpu.make_async_remote_copy(
            src_ref=src, dst_ref=recv.at[i], send_sem=send_sem.at[i], recv_sem=recv_sem.at[i],
            device_id=(r + dr, c + dc), device_id_type=MESH,
        )

    def put(name, src=None):
        copy = message(name, send.at[SLOT[name]] if src is None else src)
        there = has[MESSAGES[name]]

        @pl.when(there)
        def _():
            copy.start()

        started[name] = there, copy

    def got(name):
        dr, dc = MESSAGES[name]
        with jax.named_scope("wait_" + name):
            @pl.when(has[-dr, -dc])
            def _():
                message(name, recv.at[SLOT[name]]).wait_recv()

        return recv[SLOT[name]]

    def fill(name, value):
        send[SLOT[name]] = value

    place_copy = pltpu.make_async_remote_copy(
        src_ref=place, dst_ref=place_in, send_sem=place_send, recv_sem=place_recv,
        device_id=(r + 1, c), device_id_type=MESH,
    )
    with jax.named_scope("wait_load"):
        loads[1].wait()

    @pl.when(has[DOWN])
    def _():
        place_copy.start()

    first = {
        "t": ("obj_ht", obj.at[:, TOP, LEFT]),
        "b": ("obj_hb", obj.at[:, BOTTOM, LEFT]),
        "r": ("obj_vr", obj.at[:, TOP, RIGHT]),
    }
    for k in CFG["R1pre"]:
        put(*first[k])

    def build_tables():
        re_high, re_low, im_high, im_low = (table[i] for i in range(4))
        blocks = [
            (re_high, im_high), (re_high, im_high), (re_low, im_low),
            (-im_high, re_high), (-im_high, re_high), (-im_low, re_low),
        ]
        for b, (real, imag) in enumerate(blocks):
            span = pl.ds(b * N, N)
            right_table[span, pl.ds(0, N)] = real
            right_table[span, pl.ds(N, N)] = imag
            for half in range(2):
                left_table[pl.ds(half * N, W), span] = real[half * W : (half + 1) * W]
                left_table[pl.ds(half * N + W, W), span] = imag[half * W : (half + 1) * W]

    def turn_probe():
        for part in range(2):
            turned = pltpu.roll(probe[part], dy, 0)
            probe[part] = pltpu.roll(turned, dx, 1)

    loads[2].wait()
    build_tables()

    @pl.when(has[UP])
    def _():
        place_copy.wait_recv()

    beside_above = cols.astype(F32) < place_in[0:1, :]

    fill("obj_vl", jnp.where(beside_above, got("obj_ht"), obj[:, TOP, LEFT]))
    put("obj_vl")
    for k in CFG["R1post"]:
        put(*first[k])
    loads[3].wait()
    turn_probe()

    def put_stack(span_rows, span_cols, real, imag):
        for base, value in ((0, real), (3, imag)):
            high, low = split(value)
            for b, item in ((0, high), (1, low), (2, high)):
                stack[span_rows, pl.ds((base + b) * N + span_cols, item.shape[1])] = item

    def put_stack2(row, real, imag):
        for base, value in ((0, real), (3, imag)):
            high, low = split(value)
            for b, item in ((0, high), (1, low), (2, high)):
                stack2[pl.ds((base + b) * N + row, item.shape[0]), :] = item

    def exit_wave(half, quarter_left, quarter_right):
        span = TOP if half == 0 else BOTTOM
        for side, patch in ((0, quarter_left), (1, quarter_right)):
            lanes = pl.ds(side * W, W)
            pr, pi = probe[0, span, lanes], probe[1, span, lanes]
            put_stack(
                span, side * W,
                pr * patch[0] - pi * patch[1], pr * patch[1] + pi * patch[0],
            )

    def right_product(half):
        span = pl.ds(half * W, W)
        out = jnp.dot(stack[span, :], right_table[...], preferred_element_type=F32)
        put_stack2(half * W, out[:, :N], out[:, N:])

    def left_product(half):
        out = jnp.dot(
            left_table[pl.ds(half * N, N), :], stack2[...], preferred_element_type=F32
        )
        return out[:W], out[W:]

    def back_product(half):
        span = pl.ds(half * W, W)
        back_re, back_im = left_product(half)
        pr, pi = probe[0, span, :], probe[1, span, :]
        grad[0, span, :] = pr * back_re - pi * back_im
        grad[1, span, :] = -(pr * back_im) - pi * back_re

    def sweep(source, low_left, low_right, right_top, right_bottom):
        for k in CFG["sweep"]:
            if k == "t":
                top_right = jnp.where(below, low_right(), source[:, TOP, RIGHT])
                own = jnp.where(beside, right_top(), source[:, TOP, LEFT])
                exit_wave(0, jnp.where(below, low_left(), own), top_right)
                right_product(0)
            else:
                bottom = jnp.where(beside, right_bottom(), source[:, BOTTOM, LEFT])
                exit_wave(1, bottom, source[:, BOTTOM, RIGHT])
                right_product(1)
        for half in range(2):
            far_re, far_im = left_product(half)
            misfit = far_re * far_re + far_im * far_im - meas[pl.ds(half * W, W), :]
            put_stack(pl.ds(half * W, W), 0, misfit * far_re, -(misfit * far_im))
        for half in range(2):
            right_product(half)

    def update(old_obj, old_vel, new_obj, new_vel, span_r, span_c, gradient):
        speed = MOMENTUM * old_vel[:, span_r, span_c] + gradient
        moved = old_obj[:, span_r, span_c] - STEP * speed
        new_vel[:, span_r, span_c] = speed
        new_obj[:, span_r, span_c] = moved
        return moved

    loads[4].wait()
    sweep(
        obj, lambda: got("obj_vl"), lambda: got("obj_vr"),
        lambda: recv[SLOT["obj_ht"]], lambda: got("obj_hb"),
    )
    back_product(0)
    fill("grad_vl", jnp.where(below, grad[:, TOP, LEFT], 0.0))
    put("grad_vl")
    loads[5].wait()

    def coasting(span_r, span_c):
        return obj[:, span_r, span_c] - (STEP * MOMENTUM) * vel[:, span_r, span_c]

    def send_r():
        fill("grad_vr", jnp.where(below, grad[:, TOP, RIGHT], 0.0))
        put("grad_vr")

    def send_R():
        fill("next_vr", coasting(TOP, RIGHT) - STEP * jnp.where(below, 0.0, grad[:, TOP, RIGHT]))
        put("next_vr")

    def send_b():
        fill("grad_hb", jnp.where(beside, grad[:, BOTTOM, LEFT], 0.0))
        put("grad_hb")

    def send_B():
        fill("next_hb", coasting(BOTTOM, LEFT) - STEP * jnp.where(beside, 0.0, grad[:, BOTTOM, LEFT]))
        put("next_hb")

    sends = {"r": send_r, "R": send_R, "b": send_b, "B": send_B}
    for k in CFG["mid"]:
        if k == "|":
            back_product(1)
        else:
            sends[k]()

    above = got("grad_vl")
    across = jnp.where(beside & ~below, grad[:, TOP, LEFT], 0.0) + jnp.where(beside_above, above, 0.0)
    kept = jnp.where(below | beside, 0.0, grad[:, TOP, LEFT]) + jnp.where(beside_above, 0.0, above)
    halo[0] = across
    halo[1] = kept

    def send_h():
        fill("grad_ht", halo[0])
        put("grad_ht")

    def send_H():
        fill("next_ht", coasting(TOP, LEFT) - STEP * halo[1])
        put("next_ht")

    sends |= {"h": send_h, "H": send_H}
    for k in CFG["mid2"]:
        sends[k]()

    step_right = jnp.where(has[TO_RIGHT], STEP, 0.0)
    step_down = jnp.where(has[DOWN], STEP, 0.0)
    moving = (obj, vel, obj1, vel1)
    update(*moving, BOTTOM, RIGHT, grad[:, BOTTOM, RIGHT])
    moved = update(*moving, TOP, LEFT, halo[1] + got("grad_ht"))
    right_top = got("next_ht") - step_right * halo[0]
    halo[0] = right_top
    fill("next_vl", jnp.where(beside_above, right_top, moved))
    put("next_vl")
    update(*moving, BOTTOM, LEFT, jnp.where(beside, 0.0, grad[:, BOTTOM, LEFT]) + got("grad_hb"))
    update(*moving, TOP, RIGHT, jnp.where(below, 0.0, grad[:, TOP, RIGHT]) + got("grad_vr"))

    def low_right():
        return got("next_vr") - step_down * jnp.where(below, grad[:, TOP, RIGHT], 0.0)

    def right_bottom():
        return got("next_hb") - step_right * jnp.where(beside, grad[:, BOTTOM, LEFT], 0.0)

    sweep(obj1, lambda: got("next_vl"), low_right, lambda: halo[0], right_bottom)
    back_product(0)
    fill("last_vl", jnp.where(below, grad[:, TOP, LEFT], 0.0))
    put("last_vl")

    def last_r():
        fill("last_vr", jnp.where(below, grad[:, TOP, RIGHT], 0.0))
        put("last_vr")

    def last_b():
        fill("last_hb", jnp.where(beside, grad[:, BOTTOM, LEFT], 0.0))
        put("last_hb")

    lasts = {"r": last_r, "b": last_b, "|": lambda: back_product(1)}
    for k in CFG["R4pre"]:
        lasts[k]()
    above = got("last_vl")
    fill("last_ht", jnp.where(beside & ~below, grad[:, TOP, LEFT], 0.0) + jnp.where(beside_above, above, 0.0))
    put("last_ht")
    for k in CFG["R4post"]:
        lasts[k]()

    for there, copy in [started.pop(name) for name, _ in first.values()]:
        @pl.when(there)
        def _():
            copy.wait_send()

    stores = []
    moving = (obj1, vel1, obj, vel)

    def finish(span_r, span_c, gradient):
        update(*moving, span_r, span_c, gradient)
        for src, dst in ((obj, obj_out), (vel, vel_out)):
            copy = pltpu.make_async_copy(
                src.at[:, span_r, span_c], dst.at[:, span_r, span_c], store_sem.at[len(stores)]
            )
            copy.start()
            stores.append(copy)

    finish(BOTTOM, RIGHT, grad[:, BOTTOM, RIGHT])
    finish(TOP, RIGHT, jnp.where(below, 0.0, grad[:, TOP, RIGHT]) + got("last_vr"))
    kept = jnp.where(below | beside, 0.0, grad[:, TOP, LEFT]) + jnp.where(beside_above, 0.0, recv[SLOT["last_vl"]])
    if CFG["R4post"]:
        finish(TOP, LEFT, kept + got("last_ht"))
        finish(BOTTOM, LEFT, jnp.where(beside, 0.0, grad[:, BOTTOM, LEFT]) + got("last_hb"))
    else:
        finish(BOTTOM, LEFT, jnp.where(beside, 0.0, grad[:, BOTTOM, LEFT]) + got("last_hb"))
        finish(TOP, LEFT, kept + got("last_ht"))

    for there, copy in [*started.values(), (has[DOWN], place_copy)]:
        @pl.when(there)
        def _():
            copy.wait_send()

    for copy in stores:
        copy.wait()


def on_device(n_rows, n_cols, object_field, velocity, positions, measured, probe):
    vmem = lambda *shape: pltpu.VMEM(shape, F32)
    anywhere = pl.BlockSpec(memory_space=pl.ANY)
    count = len(MESSAGES)
    field = jax.ShapeDtypeStruct((2, N, N), F32)
    return pl.pallas_call(
        functools.partial(kernel, n_rows, n_cols),
        out_shape=(field, field),
        in_specs=[anywhere] * 6,
        out_specs=(anywhere, anywhere),
        scratch_shapes=[
            pltpu.SMEM((2,), jnp.int32),
            vmem(2, N, N), vmem(2, N, N), vmem(2, N, N), vmem(2, N, N),
            vmem(N, N), vmem(2, N, N),
            pltpu.VMEM((4, N, N), BF16),
            pltpu.VMEM((6 * N, 2 * N), BF16),
            pltpu.VMEM((2 * N, 6 * N), BF16),
            pltpu.VMEM((N, 6 * N), BF16),
            pltpu.VMEM((6 * N, N), BF16),
            vmem(2, N, N), vmem(2, 2, W, W),
            vmem(count, 2, W, W), vmem(count, 2, W, W),
            vmem(8, W), vmem(8, W),
            pltpu.SemaphoreType.DMA((6,)), pltpu.SemaphoreType.DMA((8,)),
            pltpu.SemaphoreType.DMA((count,)), pltpu.SemaphoreType.DMA((count,)),
            pltpu.SemaphoreType.DMA, pltpu.SemaphoreType.DMA,
        ],
        compiler_params=pltpu.CompilerParams(collective_id=0, has_side_effects=True),
        name="ptycho",
    )(
        positions.reshape(2), object_field, velocity, measured.reshape(N, N), probe,
        jnp.asarray(fourier_tables()),
    )


def solution(mesh):
    placed = (
        P(None, "row", "col"),
        P(None, "row", "col"),
        P("row", "col", None, None),
        P("row", "col", None, None, None),
        P(),
    )
    return jax.shard_map(
        functools.partial(on_device, mesh.shape["row"], mesh.shape["col"]),
        mesh=mesh,
        in_specs=placed,
        out_specs=(P(None, "row", "col"), P(None, "row", "col")),
        check_vma=False,
    )
```

profile of v0, /device:TPU:390, one launch (start us, length us, event | category | flops | bytes accessed | tf_op | source)
XLA Modules:
  0.0 69.7 jit_solution(14797623232129515930)
XLA Ops:
  0.6 66.3 %ptycho.1 = (f32[2,256,256]{2,1,0:T(8,128)}, f32[2,256,256]{2,1,0:T(8,128)}) custom-call(s32[2]{0:T(128)} %bitcast.3, f32[2,256,256]{2,1,0:T(8,128)} %obj_hbm.1, f32[2,256,256]{2,1,0:T(8,128)} %vel_hbm.1, f32[256,256]{1,0:T(8,128)} %bitcast.2, f32[2,256,256]{2,1,0:T(8,128)} %probe_hbm.1, bf16[4,256,256]{2,1,0:T(8,128)(2,1)} %constant.2.clone.table_hbm), custom_call_target="tpu_custom_call" | custom-call | tf_op jit(solution)/shard_map/ptycho/pallas_call | solution.py:389
  67.0 0.0 copy-start
  67.0 1.9 %copy.10 = f32[2,256,256]{2,1,0:T(8,128)} copy(f32[2,256,256]{2,1,0:T(8,128)} %get-tuple-element.4) | data formatting | bytes 1048576
  68.9 0.0 copy-done
  68.9 0.8 %copy.11 = f32[2,256,256]{2,1,0:T(8,128)} copy(f32[2,256,256]{2,1,0:T(8,128)S(1)} %copy-done) | data formatting | bytes 1048576
Async XLA Ops:
  67.0 1.9 %copy-start = (f32[2,256,256]{2,1,0:T(8,128)S(1)}, f32[2,256,256]{2,1,0:T(8,128)}, u32[]{:S(2)}) copy-start(f32[2,256,256]{2,1,0:T(8,128)} %get-tuple-element.5) | copy-start | bytes 1572868
where the time goes:
time: 69.9 us; the launch traced here: 69.7 us
  Pallas kernels  66.3 us (95%)
  local copies, waits for them, and re-layouts  2.72 us (4%)
    pallas_call x1, Pallas kernels, on_device(): pl.pallas_call(functools.partial(kernel, n_rows, n_cols), out_shape=(fiel...  66.3 us
    unnamed x4, local copies, waits for them, and re-layouts  2.72 us

commit v1 on v0

--- a/solution.py
+++ b/solution.py
@@ -1,4 +1,5 @@
 import functools
+import re
 
 import numpy as np
 
@@ -30,7 +31,11 @@
 LEFT, RIGHT = pl.ds(0, W), pl.ds(W, W)
 
 
-CFG = dict(R1pre="tr", R1post="b", mid="|bB", mid2="hHrR", R4pre="|r", R4post="b", sweep="bt")
+CFG = dict(R1pre="tb0r1b1", R1post="r0", mid="|bB", mid2="hHrR", R4pre="|r0b1", R4post="b0r1", sweep="bt")
+
+
+def order(text):
+    return [(k, int(p) if p else None) for k, p in re.findall(r"([a-zA-Z|])(\d?)", text)]
 
 
 def fourier_tables():
@@ -54,7 +59,7 @@
     obj_out, vel_out,
     pos, obj, vel, obj1, vel1, meas, probe, table, right_table, left_table,
     stack, stack2, grad, halo, recv, send, place, place_in,
-    load_sem, store_sem, send_sem, recv_sem, place_send, place_recv,
+    load_sem, send_sem, recv_sem, place_send, place_recv,
 ):
     r = lax.axis_index("row")
     c = lax.axis_index("col")
@@ -88,6 +93,59 @@
     def _():
         place_in[...] = jnp.zeros((8, W), F32)
 
+    with jax.named_scope("wait_barrier"):
+        pl.semaphore_wait(barrier, sum(there.astype(jnp.int32) for there in has.values()))
+
+    started = {}
+    filled = set()
+
+    def message(name, src):
+        dr, dc = MESSAGES[name]
+        i = SLOT[name]
+        return pltpu.make_async_remote_copy(
+            src_ref=src, dst_ref=recv.at[i], send_sem=send_sem.at[i], recv_sem=recv_sem.at[i],
+            device_id=(r + dr, c + dc), device_id_type=MESH,
+        )
+
+    def put(name, src=None, only=None):
+        copy = message(name, send.at[SLOT[name]] if src is None else src)
+        there = has[MESSAGES[name]]
+
+        @pl.when(there if only is None else there & (c % 2 == only))
+        def _():
+            copy.start()
+
+        started[name] = there, copy
+
+    def got(name):
+        dr, dc = MESSAGES[name]
+        with jax.named_scope("wait_" + name):
+            @pl.when(has[-dr, -dc])
+            def _():
+                message(name, recv.at[SLOT[name]]).wait_recv()
+
+        return recv[SLOT[name]]
+
+    def fill(name, value):
+        if name not in filled:
+            filled.add(name)
+            send[SLOT[name]] = value()
+
+    place_copy = pltpu.make_async_remote_copy(
+        src_ref=place, dst_ref=place_in, send_sem=place_send, recv_sem=place_recv,
+        device_id=(r + 1, c), device_id_type=MESH,
+    )
+    with jax.named_scope("wait_load"):
+        loads[1].wait()
+
+    first = {
+        "t": ("obj_ht", obj.at[:, TOP, LEFT]),
+        "b": ("obj_hb", obj.at[:, BOTTOM, LEFT]),
+        "r": ("obj_vr", obj.at[:, TOP, RIGHT]),
+    }
+    for k, only in order(CFG["R1pre"]):
+        put(*first[k], only)
+
     loads[0].wait()
     dy = pos[0]
     dx = pos[1]
@@ -97,59 +155,9 @@
     beside = cols < dx
     place[...] = jnp.full((8, W), dx.astype(F32))
 
-    with jax.named_scope("wait_barrier"):
-        pl.semaphore_wait(barrier, sum(there.astype(jnp.int32) for there in has.values()))
-
-    started = {}
-
-    def message(name, src):
-        dr, dc = MESSAGES[name]
-        i = SLOT[name]
-        return pltpu.make_async_remote_copy(
-            src_ref=src, dst_ref=recv.at[i], send_sem=send_sem.at[i], recv_sem=recv_sem.at[i],
-            device_id=(r + dr, c + dc), device_id_type=MESH,
-        )
-
-    def put(name, src=None):
-        copy = message(name, send.at[SLOT[name]] if src is None else src)
-        there = has[MESSAGES[name]]
-
-        @pl.when(there)
-        def _():
-            copy.start()
-
-        started[name] = there, copy
-
-    def got(name):
-        dr, dc = MESSAGES[name]
-        with jax.named_scope("wait_" + name):
-            @pl.when(has[-dr, -dc])
-            def _():
-                message(name, recv.at[SLOT[name]]).wait_recv()
-
-        return recv[SLOT[name]]
-
-    def fill(name, value):
-        send[SLOT[name]] = value
-
-    place_copy = pltpu.make_async_remote_copy(
-        src_ref=place, dst_ref=place_in, send_sem=place_send, recv_sem=place_recv,
-        device_id=(r + 1, c), device_id_type=MESH,
-    )
-    with jax.named_scope("wait_load"):
-        loads[1].wait()
-
     @pl.when(has[DOWN])
     def _():
         place_copy.start()
-
-    first = {
-        "t": ("obj_ht", obj.at[:, TOP, LEFT]),
-        "b": ("obj_hb", obj.at[:, BOTTOM, LEFT]),
-        "r": ("obj_vr", obj.at[:, TOP, RIGHT]),
-    }
-    for k in CFG["R1pre"]:
-        put(*first[k])
 
     def build_tables():
         re_high, re_low, im_high, im_low = (table[i] for i in range(4))
@@ -179,10 +187,10 @@
 
     beside_above = cols.astype(F32) < place_in[0:1, :]
 
-    fill("obj_vl", jnp.where(beside_above, got("obj_ht"), obj[:, TOP, LEFT]))
+    fill("obj_vl", lambda: jnp.where(beside_above, got("obj_ht"), obj[:, TOP, LEFT]))
     put("obj_vl")
-    for k in CFG["R1post"]:
-        put(*first[k])
+    for k, only in order(CFG["R1post"]):
+        put(*first[k], only)
     loads[3].wait()
     turn_probe()
 
@@ -257,35 +265,35 @@
         lambda: recv[SLOT["obj_ht"]], lambda: got("obj_hb"),
     )
     back_product(0)
-    fill("grad_vl", jnp.where(below, grad[:, TOP, LEFT], 0.0))
+    fill("grad_vl", lambda: jnp.where(below, grad[:, TOP, LEFT], 0.0))
     put("grad_vl")
     loads[5].wait()
 
     def coasting(span_r, span_c):
         return obj[:, span_r, span_c] - (STEP * MOMENTUM) * vel[:, span_r, span_c]
 
-    def send_r():
-        fill("grad_vr", jnp.where(below, grad[:, TOP, RIGHT], 0.0))
-        put("grad_vr")
-
-    def send_R():
-        fill("next_vr", coasting(TOP, RIGHT) - STEP * jnp.where(below, 0.0, grad[:, TOP, RIGHT]))
-        put("next_vr")
-
-    def send_b():
-        fill("grad_hb", jnp.where(beside, grad[:, BOTTOM, LEFT], 0.0))
-        put("grad_hb")
-
-    def send_B():
-        fill("next_hb", coasting(BOTTOM, LEFT) - STEP * jnp.where(beside, 0.0, grad[:, BOTTOM, LEFT]))
-        put("next_hb")
+    def send_r(only):
+        fill("grad_vr", lambda: jnp.where(below, grad[:, TOP, RIGHT], 0.0))
+        put("grad_vr", only=only)
+
+    def send_R(only):
+        fill("next_vr", lambda: coasting(TOP, RIGHT) - STEP * jnp.where(below, 0.0, grad[:, TOP, RIGHT]))
+        put("next_vr", only=only)
+
+    def send_b(only):
+        fill("grad_hb", lambda: jnp.where(beside, grad[:, BOTTOM, LEFT], 0.0))
+        put("grad_hb", only=only)
+
+    def send_B(only):
+        fill("next_hb", lambda: coasting(BOTTOM, LEFT) - STEP * jnp.where(beside, 0.0, grad[:, BOTTOM, LEFT]))
+        put("next_hb", only=only)
 
     sends = {"r": send_r, "R": send_R, "b": send_b, "B": send_B}
-    for k in CFG["mid"]:
+    for k, only in order(CFG["mid"]):
         if k == "|":
             back_product(1)
         else:
-            sends[k]()
+            sends[k](only)
 
     above = got("grad_vl")
     across = jnp.where(beside & ~below, grad[:, TOP, LEFT], 0.0) + jnp.where(beside_above, above, 0.0)
@@ -293,17 +301,17 @@
     halo[0] = across
     halo[1] = kept
 
-    def send_h():
-        fill("grad_ht", halo[0])
-        put("grad_ht")
-
-    def send_H():
-        fill("next_ht", coasting(TOP, LEFT) - STEP * halo[1])
-        put("next_ht")
+    def send_h(only):
+        fill("grad_ht", lambda: halo[0])
+        put("grad_ht", only=only)
+
+    def send_H(only):
+        fill("next_ht", lambda: coasting(TOP, LEFT) - STEP * halo[1])
+        put("next_ht", only=only)
 
     sends |= {"h": send_h, "H": send_H}
-    for k in CFG["mid2"]:
-        sends[k]()
+    for k, only in order(CFG["mid2"]):
+        sends[k](only)
 
     step_right = jnp.where(has[TO_RIGHT], STEP, 0.0)
     step_down = jnp.where(has[DOWN], STEP, 0.0)
@@ -312,7 +320,7 @@
     moved = update(*moving, TOP, LEFT, halo[1] + got("grad_ht"))
     right_top = got("next_ht") - step_right * halo[0]
     halo[0] = right_top
-    fill("next_vl", jnp.where(beside_above, right_top, moved))
+    fill("next_vl", lambda: jnp.where(beside_above, right_top, moved))
     put("next_vl")
     update(*moving, BOTTOM, LEFT, jnp.where(beside, 0.0, grad[:, BOTTOM, LEFT]) + got("grad_hb"))
     update(*moving, TOP, RIGHT, jnp.where(below, 0.0, grad[:, TOP, RIGHT]) + got("grad_vr"))
@@ -325,42 +333,30 @@
 
     sweep(obj1, lambda: got("next_vl"), low_right, lambda: halo[0], right_bottom)
     back_product(0)
-    fill("last_vl", jnp.where(below, grad[:, TOP, LEFT], 0.0))
+    fill("last_vl", lambda: jnp.where(below, grad[:, TOP, LEFT], 0.0))
     put("last_vl")
 
-    def last_r():
-        fill("last_vr", jnp.where(below, grad[:, TOP, RIGHT], 0.0))
-        put("last_vr")
-
-    def last_b():
-        fill("last_hb", jnp.where(beside, grad[:, BOTTOM, LEFT], 0.0))
-        put("last_hb")
-
-    lasts = {"r": last_r, "b": last_b, "|": lambda: back_product(1)}
-    for k in CFG["R4pre"]:
-        lasts[k]()
+    def last_r(only):
+        fill("last_vr", lambda: jnp.where(below, grad[:, TOP, RIGHT], 0.0))
+        put("last_vr", only=only)
+
+    def last_b(only):
+        fill("last_hb", lambda: jnp.where(beside, grad[:, BOTTOM, LEFT], 0.0))
+        put("last_hb", only=only)
+
+    lasts = {"r": last_r, "b": last_b, "|": lambda only: back_product(1)}
+    for k, only in order(CFG["R4pre"]):
+        lasts[k](only)
     above = got("last_vl")
-    fill("last_ht", jnp.where(beside & ~below, grad[:, TOP, LEFT], 0.0) + jnp.where(beside_above, above, 0.0))
+    fill("last_ht", lambda: jnp.where(beside & ~below, grad[:, TOP, LEFT], 0.0) + jnp.where(beside_above, above, 0.0))
     put("last_ht")
-    for k in CFG["R4post"]:
-        lasts[k]()
-
-    for there, copy in [started.pop(name) for name, _ in first.values()]:
-        @pl.when(there)
-        def _():
-            copy.wait_send()
-
-    stores = []
-    moving = (obj1, vel1, obj, vel)
+    for k, only in order(CFG["R4post"]):
+        lasts[k](only)
+
+    moving = (obj1, vel1, obj_out, vel_out)
 
     def finish(span_r, span_c, gradient):
         update(*moving, span_r, span_c, gradient)
-        for src, dst in ((obj, obj_out), (vel, vel_out)):
-            copy = pltpu.make_async_copy(
-                src.at[:, span_r, span_c], dst.at[:, span_r, span_c], store_sem.at[len(stores)]
-            )
-            copy.start()
-            stores.append(copy)
 
     finish(BOTTOM, RIGHT, grad[:, BOTTOM, RIGHT])
     finish(TOP, RIGHT, jnp.where(below, 0.0, grad[:, TOP, RIGHT]) + got("last_vr"))
@@ -377,7 +373,16 @@
         def _():
             copy.wait_send()
 
-    for copy in stores:
+
+def write_kernel(obj, vel, obj_out, vel_out, sem):
+    copies = [
+        pltpu.make_async_copy(src.at[part], dst.at[part], sem.at[2 * i + part])
+        for i, (src, dst) in enumerate([(obj, obj_out), (vel, vel_out)])
+        for part in range(2)
+    ]
+    for copy in copies:
+        copy.start()
+    for copy in copies:
         copy.wait()
 
 
@@ -385,12 +390,11 @@
     vmem = lambda *shape: pltpu.VMEM(shape, F32)
     anywhere = pl.BlockSpec(memory_space=pl.ANY)
     count = len(MESSAGES)
-    field = jax.ShapeDtypeStruct((2, N, N), F32)
-    return pl.pallas_call(
+    results = pl.pallas_call(
         functools.partial(kernel, n_rows, n_cols),
-        out_shape=(field, field),
+        out_shape=(pltpu.VMEM((2, N, N), F32), pltpu.VMEM((2, N, N), F32)),
         in_specs=[anywhere] * 6,
-        out_specs=(anywhere, anywhere),
+        out_specs=(pl.BlockSpec(memory_space=pltpu.VMEM),) * 2,
         scratch_shapes=[
             pltpu.SMEM((2,), jnp.int32),
             vmem(2, N, N), vmem(2, N, N), vmem(2, N, N), vmem(2, N, N),
@@ -403,7 +407,7 @@
             vmem(2, N, N), vmem(2, 2, W, W),
             vmem(count, 2, W, W), vmem(count, 2, W, W),
             vmem(8, W), vmem(8, W),
-            pltpu.SemaphoreType.DMA((6,)), pltpu.SemaphoreType.DMA((8,)),
+            pltpu.SemaphoreType.DMA((6,)),
             pltpu.SemaphoreType.DMA((count,)), pltpu.SemaphoreType.DMA((count,)),
             pltpu.SemaphoreType.DMA, pltpu.SemaphoreType.DMA,
         ],
@@ -413,6 +417,15 @@
         positions.reshape(2), object_field, velocity, measured.reshape(N, N), probe,
         jnp.asarray(fourier_tables()),
     )
+    field = jax.ShapeDtypeStruct((2, N, N), F32)
+    return pl.pallas_call(
+        write_kernel,
+        out_shape=(field, field),
+        in_specs=[pl.BlockSpec(memory_space=pltpu.VMEM)] * 2,
+        out_specs=(anywhere, anywhere),
+        scratch_shapes=[pltpu.SemaphoreType.DMA((4,))],
+        name="write",
+    )(*(pltpu.with_memory_space_constraint(x, pltpu.VMEM) for x in results))
 
 
 def solution(mesh):

time: 69.9 us -> 67.7 us (0.969)
  the two profiles are of different devices: /device:TPU:390 before, /device:TPU:135 now
where the time goes in v1:
time: 67.7 us; the launch traced here: 67.5 us
  Pallas kernels  66.9 us (99%)
    pallas_call x1, Pallas kernels, on_device(): pl.pallas_call(functools.partial(kernel, n_rows, n_cols), out_shape=(pltp...  65.9 us

profile of v1, /device:TPU:135, one launch (start us, length us, event | category | flops | bytes accessed | tf_op | source)
XLA Modules:
  0.0 67.5 jit_solution(1250227607985897618)
XLA Ops:
  0.6 65.9 %ptycho.1 = (f32[2,256,256]{2,1,0:T(8,128)S(1)}, f32[2,256,256]{2,1,0:T(8,128)S(1)}) custom-call(s32[2]{0:T(128)} %bitcast.3, f32[2,256,256]{2,1,0:T(8,128)} %obj_hbm.1, f32[2,256,256]{2,1,0:T(8,128)} %vel_hbm.1, f32[256,256]{1,0:T(8,128)} %bitcast.2, f32[2,256,256]{2,1,0:T(8,128)} %probe_hbm.1, bf16[4,256,256]{2,1,0:T(8,128)(2,1)} %constant.2.clone.table_hbm), custom_call_target="tpu_custom_call" | custom-call | tf_op jit(solution)/shard_map/ptycho/pallas_call | solution.py:393
  66.5 1.0 %write.1 = (f32[2,256,256]{2,1,0:T(8,128)}, f32[2,256,256]{2,1,0:T(8,128)}) custom-call(f32[2,256,256]{2,1,0:T(8,128)S(1)} %get-tuple-element.4.obj, f32[2,256,256]{2,1,0:T(8,128)S(1)} %get-tuple-element.5.vel), custom_call_target="tpu_custom_call" | custom-call | tf_op jit(solution)/shard_map/write/pallas_call | solution.py:421

commit v2 on v1

--- a/solution.py
+++ b/solution.py
@@ -31,7 +31,7 @@
 LEFT, RIGHT = pl.ds(0, W), pl.ds(W, W)
 
 
-CFG = dict(R1pre="tb0r1b1", R1post="r0", mid="|bB", mid2="hHrR", R4pre="|r0b1", R4post="b0r1", sweep="bt")
+CFG = dict(R1pre="tb0r1b1", R1post="r0", mid="|bB", mid2="hHw1rR", R4pre="|r0b1", R4post="b0r1", sweep="bt", R1x=())
 
 
 def order(text):
@@ -98,6 +98,7 @@
 
     started = {}
     filled = set()
+    flushed = {}
 
     def message(name, src):
         dr, dc = MESSAGES[name]
@@ -116,6 +117,14 @@
             copy.start()
 
         started[name] = there, copy
+
+    def flush(name, only):
+        there, copy = started[name]
+        flushed[name] = only
+
+        @pl.when(there & (c % 2 == only))
+        def _():
+            copy.wait_send()
 
     def got(name):
         dr, dc = MESSAGES[name]
@@ -186,6 +195,9 @@
         place_copy.wait_recv()
 
     beside_above = cols.astype(F32) < place_in[0:1, :]
+
+    for name in CFG["R1x"]:
+        flush(name, 0)
 
     fill("obj_vl", lambda: jnp.where(beside_above, got("obj_ht"), obj[:, TOP, LEFT]))
     put("obj_vl")
@@ -249,8 +261,13 @@
             far_re, far_im = left_product(half)
             misfit = far_re * far_re + far_im * far_im - meas[pl.ds(half * W, W), :]
             put_stack(pl.ds(half * W, W), 0, misfit * far_re, -(misfit * far_im))
-        for half in range(2):
-            right_product(half)
+        for part in range(2):
+            out = jnp.dot(
+                stack[...], right_table[:, pl.ds(part * N, N)], preferred_element_type=F32
+            )
+            high, low = split(out)
+            for b, item in ((0, high), (1, low), (2, high)):
+                stack2[pl.ds((3 * part + b) * N, N), :] = item
 
     def update(old_obj, old_vel, new_obj, new_vel, span_r, span_c, gradient):
         speed = MOMENTUM * old_vel[:, span_r, span_c] + gradient
@@ -309,7 +326,10 @@
         fill("next_ht", lambda: coasting(TOP, LEFT) - STEP * halo[1])
         put("next_ht", only=only)
 
-    sends |= {"h": send_h, "H": send_H}
+    sends |= {
+        "h": send_h, "H": send_H,
+        "w": lambda only: flush("grad_ht", only), "W": lambda only: flush("next_ht", only),
+    }
     for k, only in order(CFG["mid2"]):
         sends[k](only)
 
@@ -323,9 +343,9 @@
     fill("next_vl", lambda: jnp.where(beside_above, right_top, moved))
     put("next_vl")
     update(*moving, BOTTOM, LEFT, jnp.where(beside, 0.0, grad[:, BOTTOM, LEFT]) + got("grad_hb"))
-    update(*moving, TOP, RIGHT, jnp.where(below, 0.0, grad[:, TOP, RIGHT]) + got("grad_vr"))
 
     def low_right():
+        update(*moving, TOP, RIGHT, jnp.where(below, 0.0, grad[:, TOP, RIGHT]) + got("grad_vr"))
         return got("next_vr") - step_down * jnp.where(below, grad[:, TOP, RIGHT], 0.0)
 
     def right_bottom():
@@ -368,10 +388,14 @@
         finish(BOTTOM, LEFT, jnp.where(beside, 0.0, grad[:, BOTTOM, LEFT]) + got("last_hb"))
         finish(TOP, LEFT, kept + got("last_ht"))
 
-    for there, copy in [*started.values(), (has[DOWN], place_copy)]:
-        @pl.when(there)
+    for name, (there, copy) in started.items():
+        @pl.when(there & (c % 2 != flushed[name]) if name in flushed else there)
         def _():
             copy.wait_send()
+
+    @pl.when(has[DOWN])
+    def _():
+        place_copy.wait_send()
 
 
 def write_kernel(obj, vel, obj_out, vel_out, sem):

time: 67.7 us -> 67.2 us (level)
  the two profiles are of different devices: /device:TPU:135 before, /device:TPU:71 now
where the time goes in v2:
time: 67.2 us; the launch traced here: 67 us
  Pallas kernels  66.4 us (99%)
    pallas_call x1, Pallas kernels, on_device(): pl.pallas_call(functools.partial(kernel, n_rows, n_cols), out_shape=(pltp...  65.4 us

profile of v2, /device:TPU:71, one launch (start us, length us, event | category | flops | bytes accessed | tf_op | source)
XLA Modules:
  0.0 67.0 jit_solution(7324123626641440377)
XLA Ops:
  0.6 65.4 %ptycho.1 = (f32[2,256,256]{2,1,0:T(8,128)S(1)}, f32[2,256,256]{2,1,0:T(8,128)S(1)}) custom-call(s32[2]{0:T(128)} %bitcast.3, f32[2,256,256]{2,1,0:T(8,128)} %obj_hbm.1, f32[2,256,256]{2,1,0:T(8,128)} %vel_hbm.1, f32[256,256]{1,0:T(8,128)} %bitcast.2, f32[2,256,256]{2,1,0:T(8,128)} %probe_hbm.1, bf16[4,256,256]{2,1,0:T(8,128)(2,1)} %constant.2.clone.table_hbm), custom_call_target="tpu_custom_call" | custom-call | tf_op jit(solution)/shard_map/ptycho/pallas_call | solution.py:417
  66.0 1.0 %write.1 = (f32[2,256,256]{2,1,0:T(8,128)}, f32[2,256,256]{2,1,0:T(8,128)}) custom-call(f32[2,256,256]{2,1,0:T(8,128)S(1)} %get-tuple-element.4.obj, f32[2,256,256]{2,1,0:T(8,128)S(1)} %get-tuple-element.5.vel), custom_call_target="tpu_custom_call" | custom-call | tf_op jit(solution)/shard_map/write/pallas_call | solution.py:445

commit v3 on v2

--- a/solution.py
+++ b/solution.py
@@ -31,7 +31,7 @@
 LEFT, RIGHT = pl.ds(0, W), pl.ds(W, W)
 
 
-CFG = dict(R1pre="tb0r1b1", R1post="r0", mid="|bB", mid2="hHw1rR", R4pre="|r0b1", R4post="b0r1", sweep="bt", R1x=())
+CFG = dict(R1pre="tb0r1b1", R1post="r0", mid="|bB", mid2="hHw1W0rR", R4pre="|r0b1", R4post="b0r1", sweep="bt", R1x=("obj_ht", "obj_hb"))
 
 
 def order(text):

time: 67.2 us -> 67.1 us (level)
  no operation moved by 1% of the time
where the time goes in v3:
time: 67.1 us; the launch traced here: 66.9 us
  Pallas kernels  66.3 us (99%)
    pallas_call x1, Pallas kernels, on_device(): pl.pallas_call(functools.partial(kernel, n_rows, n_cols), out_shape=(pltp...  65.3 us

profile of v3, /device:TPU:71, one launch (start us, length us, event | category | flops | bytes accessed | tf_op | source)
XLA Modules:
  0.0 66.9 jit_solution(3335411371321135845)
XLA Ops:
  0.6 65.3 %ptycho.1 = (f32[2,256,256]{2,1,0:T(8,128)S(1)}, f32[2,256,256]{2,1,0:T(8,128)S(1)}) custom-call(s32[2]{0:T(128)} %bitcast.3, f32[2,256,256]{2,1,0:T(8,128)} %obj_hbm.1, f32[2,256,256]{2,1,0:T(8,128)} %vel_hbm.1, f32[256,256]{1,0:T(8,128)} %bitcast.2, f32[2,256,256]{2,1,0:T(8,128)} %probe_hbm.1, bf16[4,256,256]{2,1,0:T(8,128)(2,1)} %constant.2.clone.table_hbm), custom_call_target="tpu_custom_call" | custom-call | tf_op jit(solution)/shard_map/ptycho/pallas_call | solution.py:417
  65.9 1.0 %write.1 = (f32[2,256,256]{2,1,0:T(8,128)}, f32[2,256,256]{2,1,0:T(8,128)}) custom-call(f32[2,256,256]{2,1,0:T(8,128)S(1)} %get-tuple-element.4.obj, f32[2,256,256]{2,1,0:T(8,128)S(1)} %get-tuple-element.5.vel), custom_call_target="tpu_custom_call" | custom-call | tf_op jit(solution)/shard_map/write/pallas_call | solution.py:445
